TPU v7x, 256 devices: a whole 4x4x8 slice. The times are simulated.
256 devices in a mesh: row: 32 (over x, y, core), col: 8 (over z).
Axes of the slice: x: 4, y: 4, z: 8, core: 2. Of those that a mesh axis runs over, the one named last changes fastest.
Arguments:
- matrix: float32 [5120, 5120], P('row', 'col'), may hold values from -64 to 64
Outputs:
- iterate: float32 [5120, 5120], P('row', 'col')
- trace_value: float32 [2], replicated
- frobenius: float32 [2], replicated
All inputs are finite; a program needn't handle non-finite values.
Results may differ from a plain program's by a relative error of at most 0.003.
Values may be sent and summed in bfloat16 or wider, within the bound.
No kernel may reach another device: no remote copies, remote signals or barrier semaphores. Data moves between devices by JAX's collectives and lax.ppermute only.
A program may use at most 64 MiB of HBM per device.

v0:
```python
import jax
import jax.numpy as jnp
from jax import lax
from jax.sharding import Mesh
from jax.sharding import PartitionSpec as P

ITERS = 2
ROW = ("row_0", "row_1", "row_2")
ROW_COL = ("row_0", "row_1", "row_2", "col")
target = 0.0625


def from_everyone(shard, axis):
    peers = lax.axis_size(axis)
    return lax.all_to_all(
        jnp.broadcast_to(shard[None], (peers, *shard.shape)), axis, 0, 0, tiled=True
    )


def in_order(pieces, dim):
    shape = list(pieces.shape[1:])
    shape[dim] *= pieces.shape[0]
    return jnp.moveaxis(pieces, 0, dim).reshape(shape)


def collect(shard, axis, dim):
    pieces = from_everyone(shard, axis)
    return in_order(pieces, dim)


def over_axes(shard, axes):
    for axis in axes:
        shard = lax.psum(shard, axis)
    return shard


def add_rows(portion, right_panel):
    return jnp.dot(portion, right_panel, preferred_element_type=jnp.float32)


def on_device(matrix):
    rounded = matrix.astype(jnp.bfloat16)
    current = rounded.astype(jnp.float32)
    row_ids = lax.axis_index(ROW) * matrix.shape[0] + lax.broadcasted_iota(
        jnp.int32, matrix.shape, 0
    )
    col_ids = lax.axis_index("col") * matrix.shape[1] + lax.broadcasted_iota(
        jnp.int32, matrix.shape, 1
    )
    on_diagonal = row_ids == col_ids
    traces = []
    norms = []
    for step in range(ITERS):
        row_panel = collect(rounded, "col", 1)
        if step == 0:
            order_full = row_panel.shape[1]
            squares = over_axes(jnp.sum(current * current), ROW_COL)
            scale = target * order_full / (squares + 1e-06)
            root = jnp.sqrt(scale)
        else:
            scale = jnp.float32(1.0)
            root = jnp.float32(1.0)
        kept_panel = lax.all_gather(rounded, ROW, axis=0, tiled=True)
        product = jnp.dot(row_panel, kept_panel, preferred_element_type=jnp.float32)
        squared = (product * scale).astype(jnp.bfloat16)
        cubic_part = add_rows(
            lax.all_gather(squared, "col", axis=1, tiled=True), right_panel=kept_panel
        )
        current = root * (1.5 * current - 0.5 * cubic_part)
        rounded = current.astype(jnp.bfloat16)
        diagonal_part = jnp.sum(jnp.where(on_diagonal, current, 0.0))
        square_part = jnp.sum(current * current)
        trace_now, total_now = (over_axes(diagonal_part, ROW_COL), over_axes(square_part, ROW_COL))
        traces.append(trace_now)
        norms.append(jnp.sqrt(total_now))
    return (current, jnp.stack(traces), jnp.stack(norms))


def solution(mesh):
    split = Mesh(
        mesh.devices.reshape(4, 4, 2, mesh.shape["col"]), ("row_0", "row_1", "row_2", "col")
    )
    return jax.shard_map(
        on_device,
        mesh=split,
        in_specs=(P(ROW, "col"),),
        out_specs=(P(ROW, "col"), P(), P()),
        check_vma=False,
    )
```

profile of v0, /device:TPU:32, one launch (start us, length us, event | category | flops | bytes accessed | tf_op | source)
XLA Modules:
  0.0 274.8 jit_solution(13605825605742799116)
XLA Ops:
  7.2 0.0 all-gather.5.cloned.1.call-start
  7.2 2.3 fusion.4
  9.5 0.0 all-gather.5.cloned.1.call-update
  9.5 2.2 broadcast_in_dim.9
  11.8 8.6 %all-to-all-start = ((bf16[8,160,640]{2,1,0:T(8,128)(2,1)}), bf16[8,160,640]{2,1,0:T(8,128)(2,1)S(1)}, u32[]{:S(2)}, u32[]{:S(2)}) async-start(bf16[8,160,640]{2,1,0:T(8,128)(2,1)} %broadcast_in_dim.9), calls=%async_computation | async-start | bytes 3276800 | tf_op jit(solution)/shard_map/all_to_all | solution.py:15
  20.4 11.1 %psum.140 = f32[]{:T(128)} all-reduce(f32[]{:T(128)} %get-tuple-element.23), channel_id=1, replica_groups=mesh['row_0'=4,'row_1'=4,'row_2'=2,'col'=8] {'row_0'}, use_global_device_ids=true, to_apply=%region_1.0 | all-reduce | flops 1 | bytes 8 | tf_op jit(solution)/shard_map/psum | solution.py:33
  31.5 11.4 %psum.141 = f32[]{:T(128)} all-reduce(f32[]{:T(128)} %psum.140), channel_id=1, replica_groups=mesh['row_0'=4,'row_1'=4,'row_2'=2,'col'=8] {'row_1'}, use_global_device_ids=true, to_apply=%region_2.0 | all-reduce | flops 1 | bytes 8 | tf_op jit(solution)/shard_map/psum | solution.py:33
  42.8 3.1 %psum.142 = f32[]{:T(128)} all-reduce(f32[]{:T(128)} %psum.141), channel_id=1, replica_groups=mesh['row_0'=4,'row_1'=4,'row_2'=2,'col'=8] {'row_2'}, use_global_device_ids=true, to_apply=%region_3.0 | all-reduce | flops 1 | bytes 8 | tf_op jit(solution)/shard_map/psum | solution.py:33
  45.9 20.6 %psum.143 = f32[]{:T(128)} all-reduce(f32[]{:T(128)} %psum.142), channel_id=1, replica_groups=mesh['row_0'=4,'row_1'=4,'row_2'=2,'col'=8] {'col'}, use_global_device_ids=true, to_apply=%region_4.0 | all-reduce | flops 1 | bytes 8 | tf_op jit(solution)/shard_map/psum | solution.py:33
  67.2 0.0 all-to-all-done
  67.2 0.2 copy.6
  67.5 0.7 all-gather.5.cloned.1.call-done
  68.2 5.0 %fusion.3 = bf16[160,640]{1,0:T(8,128)(2,1)} fusion(bf16[160,5120]{1,0:T(8,128)(2,1)S(1)} %bitcast.18, bf16[5120,640]{1,0:T(8,128)(2,1)} %all-gather.5.cloned.1.call-done, f32[]{:T(128)S(6)} %div.3), kind=kOutput, calls=%fused_computation.6 | convolution fusion | flops 1048780800 | bytes 8396804 | tf_op jit(solution)/shard_map/dot_general | solution.py:64
  73.2 0.0 all-gather.7.cloned.1.call-update
  73.2 0.0 all-gather.9.cloned.1.call-start
  73.3 41.0 %all-gather.7.cloned.1.call-done = bf16[160,5120]{1,0:T(8,128)(2,1)} async-done(((bf16[160,640]{1,0:T(8,128)(2,1)}), bf16[160,5120]{1,0:T(8,128)(2,1)}) %all-gather.7.cloned.1.call-update) | async-done | bytes 1638416 | tf_op jit(solution)/shard_map/all_gather | solution.py:67
  114.3 6.1 %multiply_reduce_fusion.1 = (f32[]{:T(128)}, f32[]{:T(128)}, bf16[160,640]{1,0:T(8,128)(2,1)}, f32[160,640]{1,0:T(8,128)S(1)}) fusion(s32[640]{0:T(1024)S(1)} %iota_add_fusion, s32[160]{0:T(256)S(1)} %iota_add_fusion.1, bf16[160,5120]{1,0:T(8,128)(2,1)} %all-gather.7.cloned.1.call-done, bf16[5120,640]{1,0:T(8,128)(2,1)} %all-gather.5.cloned.1.call-done, ...), kind=kOutput, calls=%fused_computation.16 | convolution fusion | flops 1049702400 | bytes 9014412 | tf_op jit(solution)/shard_map/dot_general | solution.py:38
  120.5 0.0 all-gather.9.cloned.1.call-update
  120.5 0.0 all-gather.11.cloned.1.call-start
  120.5 1.1 broadcast_in_dim.18
  121.6 40.6 %all_to_all.10 = bf16[8,160,640]{2,1,0:T(8,128)(2,1)S(1)} all-to-all(bf16[8,160,640]{2,1,0:T(8,128)(2,1)S(1)} %broadcast_in_dim.18), channel_id=1, replica_groups=mesh['row_0'=4,'row_1'=4,'row_2'=2,'col'=8] {'col'}, dimensions={0} | all-to-all | bytes 3276800 | tf_op jit(solution)/shard_map/all_to_all | solution.py:15
  162.2 0.2 copy.7
  162.4 11.6 %all-gather.9.cloned.1.call-done = bf16[5120,640]{1,0:T(8,128)(2,1)} async-done(((bf16[160,640]{1,0:T(8,128)(2,1)}), bf16[5120,640]{1,0:T(8,128)(2,1)}) %all-gather.9.cloned.1.call-update) | async-done | bytes 6553616 | tf_op jit(solution)/shard_map/all_gather | solution.py:63
  174.0 5.0 %convolution_convert_fusion = bf16[160,640]{1,0:T(8,128)(2,1)} fusion(bf16[160,5120]{1,0:T(8,128)(2,1)S(1)} %bitcast.19, bf16[5120,640]{1,0:T(8,128)(2,1)} %all-gather.9.cloned.1.call-done), kind=kOutput, calls=%fused_computation.7 | convolution fusion | flops 1048678400 | bytes 8396800 | tf_op jit(solution)/shard_map/dot_general | solution.py:64
  179.0 0.0 all-gather.11.cloned.1.call-update
  179.0 38.3 %all-gather.11.cloned.1.call-done = bf16[160,5120]{1,0:T(8,128)(2,1)} async-done(((bf16[160,640]{1,0:T(8,128)(2,1)}), bf16[160,5120]{1,0:T(8,128)(2,1)}) %all-gather.11.cloned.1.call-update) | async-done | bytes 1638416 | tf_op jit(solution)/shard_map/all_gather | solution.py:67
  217.3 6.2 %multiply_reduce_fusion = (f32[]{:T(128)}, f32[]{:T(128)}, f32[160,640]{1,0:T(8,128)}) fusion(s32[640]{0:T(1024)S(1)} %iota_add_fusion, s32[160]{0:T(256)S(1)} %iota_add_fusion.1, bf16[160,5120]{1,0:T(8,128)(2,1)} %all-gather.11.cloned.1.call-done, bf16[5120,640]{1,0:T(8,128)(2,1)} %all-gather.9.cloned.1.call-done, f32[160,640]{1,0:T(8,128)S(1)} %get-tuple-element.26), kind=kOutput, calls=%fused_computation.15 | convolution fusion | flops 1049395200 | bytes 9014408 | tf_op jit(solution)/shard_map/dot_general | solution.py:38
  223.5 11.1 %all-reduce.2 = (f32[]{:T(128)}, f32[]{:T(128)}, f32[]{:T(128)}, f32[]{:T(128)}) all-reduce(f32[]{:T(128)} %get-tuple-element.6, f32[]{:T(128)} %get-tuple-element.4, f32[]{:T(128)} %get-tuple-element.5, f32[]{:T(128)} %get-tuple-element.3), channel_id=1, replica_groups=mesh['row_0'=4,'row_1'=4,'row_2'=2,'col'=8] {'row_0'}, use_global_device_ids=true, to_apply=%region_11.12 | all-reduce | flops 4 | bytes 32 | tf_op jit(solution)/shard_map/psum | solution.py:33
  234.6 11.1 %all-reduce.1 = (f32[]{:T(128)}, f32[]{:T(128)}, f32[]{:T(128)}, f32[]{:T(128)}) all-reduce(f32[]{:T(128)} %get-tuple-element.15, f32[]{:T(128)} %get-tuple-element.16, f32[]{:T(128)} %get-tuple-element.17, f32[]{:T(128)} %get-tuple-element.18), channel_id=1, replica_groups=mesh['row_0'=4,'row_1'=4,'row_2'=2,'col'=8] {'row_1'}, use_global_device_ids=true, to_apply=%region_12.13 | all-reduce | flops 4 | bytes 32 | tf_op jit(solution)/shard_map/psum | solution.py:33
  245.7 3.2 %all-reduce.3 = (f32[]{:T(128)}, f32[]{:T(128)}, f32[]{:T(128)}, f32[]{:T(128)}) all-reduce(f32[]{:T(128)} %get-tuple-element.11, f32[]{:T(128)} %get-tuple-element.12, f32[]{:T(128)} %get-tuple-element.13, f32[]{:T(128)} %get-tuple-element.14), channel_id=1, replica_groups=mesh['row_0'=4,'row_1'=4,'row_2'=2,'col'=8] {'row_2'}, use_global_device_ids=true, to_apply=%region_13.14 | all-reduce | flops 4 | bytes 32 | tf_op jit(solution)/shard_map/psum | solution.py:33
  248.9 16.1 %all-reduce = (f32[1]{0:T(128)}, f32[1]{0:T(128)}, f32[]{:T(128)}, f32[]{:T(128)}) all-reduce(f32[1]{0:T(128)} %bitcast.3, f32[1]{0:T(128)} %bitcast.2, f32[]{:T(128)} %get-tuple-element.21, f32[]{:T(128)} %get-tuple-element.22), channel_id=1, replica_groups=mesh['row_0'=4,'row_1'=4,'row_2'=2,'col'=8] {'col'}, use_global_device_ids=true, to_apply=%region_14.15 | all-reduce | flops 4 | bytes 32 | tf_op jit(solution)/shard_map/psum | solution.py:33
  266.4 1.9 pad_maximum_fusion
  (5 shorter events, 0.0 us)
Async XLA Ops:
  7.2 61.0 %all-gather.5.cloned.1.call-start = ((), (), s32[]{:S(2)}) async-start(), calls=%async_computation.2 | async-start | bytes 6758400 | tf_op jit(solution)/shard_map/all_gather | solution.py:63
  11.8 55.4 %all-to-all-start = ((bf16[8,160,640]{2,1,0:T(8,128)(2,1)}), bf16[8,160,640]{2,1,0:T(8,128)(2,1)S(1)}, u32[]{:S(2)}, u32[]{:S(2)}) async-start(bf16[8,160,640]{2,1,0:T(8,128)(2,1)} %broadcast_in_dim.9), calls=%async_computation | async-start | bytes 3276800 | tf_op jit(solution)/shard_map/all_to_all | solution.py:15
  20.3 94.0 %all-gather.7.cloned.1.call-start = ((), (), s32[]{:S(2)}) async-start(), calls=%async_computation.3 | async-start | bytes 1843200 | tf_op jit(solution)/shard_map/all_gather | solution.py:67
  68.2 46.2 %copy-start = (bf16[160,640]{1,0:T(8,128)(2,1)S(1)}, bf16[160,640]{1,0:T(8,128)(2,1)}, u32[]{:S(2)}) copy-start(bf16[160,640]{1,0:T(8,128)(2,1)} %get-tuple-element.24) | copy-start | bytes 614404
  73.2 100.8 %all-gather.9.cloned.1.call-start = ((), (), s32[]{:S(2)}) async-start(), calls=%async_computation.4 | async-start | bytes 6758400 | tf_op jit(solution)/shard_map/all_gather | solution.py:63
  120.5 96.8 %all-gather.11.cloned.1.call-start = ((), (), s32[]{:S(2)}) async-start(), calls=%async_computation.5 | async-start | bytes 1843200 | tf_op jit(solution)/shard_map/all_gather | solution.py:67
Sparse Core Ops, SparseCore 0:
  11.1 57.0 all-gather.4
  73.3 40.9 all-gather.6
  120.6 53.3 all-gather.8
  179.2 38.0 all-gather.10
where the time goes:
time: 275 us
  blocking collectives  128 us (47%)
  waiting for transfers between devices  91.6 us (33%)
  matrix products  22.3 us (8%)
  between operations  15.9 us (6%)
  starting transfers between devices  8.69 us (3%)
  other arithmetic  4.18 us (2%)
  local copies, waits for them, and re-layouts  3.75 us (1%)
    psum x8, blocking collectives, over_axes(): shard = lax.psum(shard, axis)  87.7 us
    all_gather x2, waiting for transfers between devices, on_device(): lax.all_gather(squared, 'col', axis=1, tiled=True)  79.2 us
    all_to_all x1, blocking collectives, from_everyone(): lax.all_to_all(jnp.broadcast_to(shard[None], (peers, *shard.shape)), axis...  40.6 us
    dot_general x2, matrix products, add_rows(): return jnp.dot(portion, right_panel, preferred_element_type=jnp.float32)  12.3 us
    all_gather x2, waiting for transfers between devices, on_device(): kept_panel = lax.all_gather(rounded, ROW, axis=0, tiled=True)  12.3 us
    dot_general x2, matrix products, on_device(): product = jnp.dot(row_panel, kept_panel, preferred_element_type=jnp.float32)  10 us
    all_to_all x1, starting transfers between devices, from_everyone(): lax.all_to_all(jnp.broadcast_to(shard[None], (peers, *shard.shape)), axis...  8.57 us
  transfers between devices with their start and end apart: 5, of which 4 were waited for; matrix products, arithmetic and copies ran while one was open for 1% of the time, Pallas kernels for 0%

commit v1 on v0

--- a/solution.py
+++ b/solution.py
@@ -8,6 +8,25 @@
 ROW = ("row_0", "row_1", "row_2")
 ROW_COL = ("row_0", "row_1", "row_2", "col")
 target = 0.0625
+
+
+def ring_gather(x, axis, dim):
+    size, index, rows = (lax.axis_size(axis), lax.axis_index(axis), x.shape[dim])
+    forward = [(i, (i + 1) % size) for i in range(size)]
+    left = [(i, (i - 1) % size) for i in range(size)]
+    out = jnp.zeros((*x.shape[:dim], size * rows, *x.shape[dim + 1 :]), x.dtype)
+    out = lax.dynamic_update_slice_in_dim(out, x, index * rows, axis=dim)
+    from_left = from_right = x
+    middle = size // 2
+    for hop in range(1, middle + 1):
+        from_left = lax.ppermute(from_left, axis, forward)
+        out = lax.dynamic_update_slice_in_dim(out, from_left, (index - hop) % size * rows, axis=dim)
+        if hop < size - middle:
+            from_right = lax.ppermute(from_right, axis, left)
+            out = lax.dynamic_update_slice_in_dim(
+                out, from_right, (index + hop) % size * rows, axis=dim
+            )
+    return out
 
 
 def from_everyone(shard, axis):
@@ -63,9 +82,7 @@
         kept_panel = lax.all_gather(rounded, ROW, axis=0, tiled=True)
         product = jnp.dot(row_panel, kept_panel, preferred_element_type=jnp.float32)
         squared = (product * scale).astype(jnp.bfloat16)
-        cubic_part = add_rows(
-            lax.all_gather(squared, "col", axis=1, tiled=True), right_panel=kept_panel
-        )
+        cubic_part = add_rows(ring_gather(squared, "col", 1), right_panel=kept_panel)
         current = root * (1.5 * current - 0.5 * cubic_part)
         rounded = current.astype(jnp.bfloat16)
         diagonal_part = jnp.sum(jnp.where(on_diagonal, current, 0.0))

time: 275 us -> 251 us (0.913)
  waiting for transfers between devices: 91.6 us -> 54.2 us
  starting transfers between devices: 8.69 us -> 23.3 us
  matrix products: 22.3 us -> 14.6 us
  blocking collectives: 128 us -> 134 us
    all_gather x2 -> x0, waiting for transfers between devices: 79.2 us -> none  [on_device(): lax.all_gather(squared, 'col', axis=1, tiled=True)]
    ppermute x0 -> x14, waiting for transfers between devices: none -> 40.2 us  [the longest x8 37.4 us: ring_gather(): from_left = lax.ppermute(from_left, axis, forward)]
    ppermute x0 -> x14, starting transfers between devices: none -> 14.7 us  [the longest x8 10.6 us: ring_gather(): from_left = lax.ppermute(from_left, axis, forward)]
    dot_general x2, matrix products: 12.3 us -> 5.65 us  [add_rows(): return jnp.dot(portion, right_panel, preferred_element_type=jnp.float32)]
    all_to_all x1, blocking collectives: 40.6 us -> 45.8 us  [from_everyone(): lax.all_to_all(jnp.broadcast_to(shard[None], (peers, *shard.shape)), axis...]
  transfers between devices with their start and end apart: 5 -> 17, of which waited for: 4 -> 14; matrix products, arithmetic and copies ran while one was open for 1% -> 2% of each run, Pallas kernels for 0% -> 0%
where the time goes in v1:
time: 251 us
  blocking collectives  134 us (53%)
  waiting for transfers between devices  54.2 us (22%)
  starting transfers between devices  23.3 us (9%)
  between operations  16.5 us (7%)
  matrix products  14.6 us (6%)
  local copies, waits for them, and re-layouts  4.53 us (2%)
  other arithmetic  4.09 us (2%)
    psum x8, blocking collectives, over_axes(): shard = lax.psum(shard, axis)  87.7 us
    all_to_all x1, blocking collectives, from_everyone(): lax.all_to_all(jnp.broadcast_to(shard[None], (peers, *shard.shape)), axis...  45.8 us
    ppermute x8, waiting for transfers between devices, ring_gather(): from_left = lax.ppermute(from_left, axis, forward)  37.4 us
    all_gather x2, waiting for transfers between devices, on_device(): kept_panel = lax.all_gather(rounded, ROW, axis=0, tiled=True)  14 us
    ppermute x8, starting transfers between devices, ring_gather(): from_left = lax.ppermute(from_left, axis, forward)  10.6 us
    dot_general x2, matrix products, on_device(): product = jnp.dot(row_panel, kept_panel, preferred_element_type=jnp.float32)  8.96 us
    all_to_all x1, starting transfers between devices, from_everyone(): lax.all_to_all(jnp.broadcast_to(shard[None], (peers, *shard.shape)), axis...  8.57 us
    dot_general x2, matrix products, add_rows(): return jnp.dot(portion, right_panel, preferred_element_type=jnp.float32)  5.65 us
  transfers between devices with their start and end apart: 17, of which 14 were waited for; matrix products, arithmetic and copies ran while one was open for 2% of the time, Pallas kernels for 0%

profile of v1, /device:TPU:32, one launch (start us, length us, event | category | flops | bytes accessed | tf_op | source)
XLA Modules:
  0.0 250.7 jit_solution(10463118430767447587)
XLA Ops:
  7.2 2.3 fusion.3
  9.5 2.2 broadcast_in_dim.9
  11.8 8.6 %all-to-all-start = ((bf16[8,160,640]{2,1,0:T(8,128)(2,1)}), bf16[8,160,640]{2,1,0:T(8,128)(2,1)S(1)}, u32[]{:S(2)}, u32[]{:S(2)}) async-start(bf16[8,160,640]{2,1,0:T(8,128)(2,1)} %broadcast_in_dim.9), calls=%async_computation | async-start | bytes 3276800 | tf_op jit(solution)/shard_map/all_to_all | solution.py:34
  20.4 11.1 %psum.140 = f32[]{:T(128)} all-reduce(f32[]{:T(128)} %get-tuple-element.23), channel_id=1, replica_groups=mesh['row_0'=4,'row_1'=4,'row_2'=2,'col'=8] {'row_0'}, use_global_device_ids=true, to_apply=%region_1.0 | all-reduce | flops 1 | bytes 8 | tf_op jit(solution)/shard_map/psum | solution.py:52
  31.5 11.4 %psum.141 = f32[]{:T(128)} all-reduce(f32[]{:T(128)} %psum.140), channel_id=1, replica_groups=mesh['row_0'=4,'row_1'=4,'row_2'=2,'col'=8] {'row_1'}, use_global_device_ids=true, to_apply=%region_2.0 | all-reduce | flops 1 | bytes 8 | tf_op jit(solution)/shard_map/psum | solution.py:52
  42.8 3.1 %psum.142 = f32[]{:T(128)} all-reduce(f32[]{:T(128)} %psum.141), channel_id=1, replica_groups=mesh['row_0'=4,'row_1'=4,'row_2'=2,'col'=8] {'row_2'}, use_global_device_ids=true, to_apply=%region_3.0 | all-reduce | flops 1 | bytes 8 | tf_op jit(solution)/shard_map/psum | solution.py:52
  45.9 20.6 %psum.143 = f32[]{:T(128)} all-reduce(f32[]{:T(128)} %psum.142), channel_id=1, replica_groups=mesh['row_0'=4,'row_1'=4,'row_2'=2,'col'=8] {'col'}, use_global_device_ids=true, to_apply=%region_4.0 | all-reduce | flops 1 | bytes 8 | tf_op jit(solution)/shard_map/psum | solution.py:52
  68.3 4.5 %constant_dynamic-update-slice_fusion.15 = (bf16[160,5120]{1,0:T(8,128)(2,1)S(1)}, bf16[160,640]{1,0:T(8,128)(2,1)S(1)}) fusion(bf16[160,5120]{1,0:T(8,128)(2,1)S(1)} %broadcast.23.clone, s32[]{:T(128)S(6)} %select_n.84, f32[]{:T(128)S(6)} %div.3, bf16[160,5120]{1,0:T(8,128)(2,1)S(1)} %bitcast.22, bf16[5120,640]{1,0:T(8,128)(2,1)} %all-gather.3.cloned.1.call-done), kind=kOutput, calls=%fused_computation.33 | convolution fusion | flops 1048780800 | bytes 8601608 | tf_op jit(solution)/shard_map/dot_general | solution.py:83
  72.8 1.8 collective-permute-start
  75.0 5.2 %collective-permute-done = bf16[160,640]{1,0:T(8,128)(2,1)S(1)} collective-permute-done((bf16[160,640]{1,0:T(8,128)(2,1)S(1)}, bf16[160,640]{1,0:T(8,128)(2,1)S(1)}, u32[]{:S(2)}, u32[]{:S(2)}) %collective-permute-start) | collective-permute-done | bytes 204832 | tf_op jit(solution)/shard_map/ppermute | solution.py:22
  80.1 1.6 collective-permute-start.2
  82.2 4.2 %collective-permute-done.2 = bf16[160,640]{1,0:T(8,128)(2,1)S(1)} collective-permute-done((bf16[160,640]{1,0:T(8,128)(2,1)S(1)}, bf16[160,640]{1,0:T(8,128)(2,1)S(1)}, u32[]{:S(2)}, u32[]{:S(2)}) %collective-permute-start.2) | collective-permute-done | bytes 204832 | tf_op jit(solution)/shard_map/ppermute | solution.py:22
  86.5 1.4 collective-permute-start.4
  89.2 3.6 %collective-permute-done.4 = bf16[160,640]{1,0:T(8,128)(2,1)S(1)} collective-permute-done((bf16[160,640]{1,0:T(8,128)(2,1)S(1)}, bf16[160,640]{1,0:T(8,128)(2,1)S(1)}, u32[]{:S(2)}, u32[]{:S(2)}) %collective-permute-start.4) | collective-permute-done | bytes 204832 | tf_op jit(solution)/shard_map/ppermute | solution.py:22
  95.0 5.0 %collective-permute-done.6 = bf16[160,640]{1,0:T(8,128)(2,1)S(1)} collective-permute-done((bf16[160,640]{1,0:T(8,128)(2,1)S(1)}, bf16[160,640]{1,0:T(8,128)(2,1)S(1)}, u32[]{:S(2)}, u32[]{:S(2)}) %collective-permute-start.6) | collective-permute-done | bytes 204832 | tf_op jit(solution)/shard_map/ppermute | solution.py:22
  100.1 2.8 %multiply_reduce_fusion.1 = (f32[]{:T(128)}, f32[]{:T(128)}, bf16[160,640]{1,0:T(8,128)(2,1)}, f32[160,640]{1,0:T(8,128)S(1)}) fusion(s32[640]{0:T(1024)S(1)} %iota_add_fusion, s32[160]{0:T(256)S(1)} %iota_add_fusion.1, bf16[160,5120]{1,0:T(8,128)(2,1)S(1)} %constant_dynamic-update-slice_fusion.8, bf16[5120,640]{1,0:T(8,128)(2,1)S(1)} %bitcast.21, ...), kind=kOutput, calls=%fused_computation.15 | convolution fusion | flops 1049702400 | bytes 9014412 | tf_op jit(solution)/shard_map/dot_general | solution.py:57
  104.1 45.8 %all_to_all.10 = bf16[8,160,640]{2,1,0:T(8,128)(2,1)S(1)} all-to-all(bf16[8,160,640]{2,1,0:T(8,128)(2,1)S(1)} %broadcast_in_dim.18), channel_id=1, replica_groups=mesh['row_0'=4,'row_1'=4,'row_2'=2,'col'=8] {'col'}, dimensions={0} | all-to-all | bytes 3276800 | tf_op jit(solution)/shard_map/all_to_all | solution.py:34
  150.1 13.4 %all-gather.5.cloned.1.call-done = bf16[5120,640]{1,0:T(8,128)(2,1)} async-done(((bf16[160,640]{1,0:T(8,128)(2,1)}), bf16[5120,640]{1,0:T(8,128)(2,1)}) %all-gather.5.cloned.1.call-update) | async-done | bytes 6553616 | tf_op jit(solution)/shard_map/all_gather | solution.py:82
  163.6 4.5 %constant_dynamic-update-slice_fusion.7 = (bf16[160,5120]{1,0:T(8,128)(2,1)S(1)}, bf16[160,640]{1,0:T(8,128)(2,1)S(1)}) fusion(bf16[160,5120]{1,0:T(8,128)(2,1)S(1)} %broadcast.23, s32[]{:T(128)S(6)} %select_n.84, bf16[160,5120]{1,0:T(8,128)(2,1)S(1)} %bitcast.23, bf16[5120,640]{1,0:T(8,128)(2,1)} %all-gather.5.cloned.1.call-done), kind=kOutput, calls=%fused_computation.25 | convolution fusion | flops 1048678400 | bytes 8601604 | tf_op jit(solution)/shard_map/dot_general | solution.py:83
  168.1 1.8 collective-permute-start.7
  170.4 5.2 %collective-permute-done.7 = bf16[160,640]{1,0:T(8,128)(2,1)S(1)} collective-permute-done((bf16[160,640]{1,0:T(8,128)(2,1)S(1)}, bf16[160,640]{1,0:T(8,128)(2,1)S(1)}, u32[]{:S(2)}, u32[]{:S(2)}) %collective-permute-start.7) | collective-permute-done | bytes 204832 | tf_op jit(solution)/shard_map/ppermute | solution.py:22
  175.6 1.6 collective-permute-start.9
  177.7 4.8 %collective-permute-done.9 = bf16[160,640]{1,0:T(8,128)(2,1)S(1)} collective-permute-done((bf16[160,640]{1,0:T(8,128)(2,1)S(1)}, bf16[160,640]{1,0:T(8,128)(2,1)S(1)}, u32[]{:S(2)}, u32[]{:S(2)}) %collective-permute-start.9) | collective-permute-done | bytes 204832 | tf_op jit(solution)/shard_map/ppermute | solution.py:22
  184.1 1.4 collective-permute-start.12
  185.6 3.9 %collective-permute-done.11 = bf16[160,640]{1,0:T(8,128)(2,1)S(1)} collective-permute-done((bf16[160,640]{1,0:T(8,128)(2,1)S(1)}, bf16[160,640]{1,0:T(8,128)(2,1)S(1)}, u32[]{:S(2)}, u32[]{:S(2)}) %collective-permute-start.11) | collective-permute-done | bytes 204832 | tf_op jit(solution)/shard_map/ppermute | solution.py:22
  190.8 5.4 %collective-permute-done.13 = bf16[160,640]{1,0:T(8,128)(2,1)S(1)} collective-permute-done((bf16[160,640]{1,0:T(8,128)(2,1)S(1)}, bf16[160,640]{1,0:T(8,128)(2,1)S(1)}, u32[]{:S(2)}, u32[]{:S(2)}) %collective-permute-start.13) | collective-permute-done | bytes 204832 | tf_op jit(solution)/shard_map/ppermute | solution.py:22
  196.3 2.8 %multiply_reduce_fusion = (f32[]{:T(128)}, f32[]{:T(128)}, f32[160,640]{1,0:T(8,128)}) fusion(s32[640]{0:T(1024)S(1)} %iota_add_fusion, s32[160]{0:T(256)S(1)} %iota_add_fusion.1, bf16[160,5120]{1,0:T(8,128)(2,1)S(1)} %constant_dynamic-update-slice_fusion, bf16[5120,640]{1,0:T(8,128)(2,1)S(1)} %bitcast.19, f32[160,640]{1,0:T(8,128)S(1)} %get-tuple-element.28), kind=kOutput, calls=%fused_computation.14 | convolution fusion | flops 1049395200 | bytes 9014408 | tf_op jit(solution)/shard_map/dot_general | solution.py:57
  199.1 10.2 %all-reduce.2 = (f32[]{:T(128)}, f32[]{:T(128)}, f32[]{:T(128)}, f32[]{:T(128)}) all-reduce(f32[]{:T(128)} %get-tuple-element.6, f32[]{:T(128)} %get-tuple-element.4, f32[]{:T(128)} %get-tuple-element.5, f32[]{:T(128)} %get-tuple-element.3), channel_id=1, replica_groups=mesh['row_0'=4,'row_1'=4,'row_2'=2,'col'=8] {'row_0'}, use_global_device_ids=true, to_apply=%region_11.12 | all-reduce | flops 4 | bytes 32 | tf_op jit(solution)/shard_map/psum | solution.py:52
  209.3 9.9 %all-reduce.1 = (f32[]{:T(128)}, f32[]{:T(128)}, f32[]{:T(128)}, f32[]{:T(128)}) all-reduce(f32[]{:T(128)} %get-tuple-element.15, f32[]{:T(128)} %get-tuple-element.16, f32[]{:T(128)} %get-tuple-element.17, f32[]{:T(128)} %get-tuple-element.18), channel_id=1, replica_groups=mesh['row_0'=4,'row_1'=4,'row_2'=2,'col'=8] {'row_1'}, use_global_device_ids=true, to_apply=%region_12.13 | all-reduce | flops 4 | bytes 32 | tf_op jit(solution)/shard_map/psum | solution.py:52
  219.2 3.1 %all-reduce.3 = (f32[]{:T(128)}, f32[]{:T(128)}, f32[]{:T(128)}, f32[]{:T(128)}) all-reduce(f32[]{:T(128)} %get-tuple-element.11, f32[]{:T(128)} %get-tuple-element.12, f32[]{:T(128)} %get-tuple-element.13, f32[]{:T(128)} %get-tuple-element.14), channel_id=1, replica_groups=mesh['row_0'=4,'row_1'=4,'row_2'=2,'col'=8] {'row_2'}, use_global_device_ids=true, to_apply=%region_13.14 | all-reduce | flops 4 | bytes 32 | tf_op jit(solution)/shard_map/psum | solution.py:52
  222.3 18.4 %all-reduce = (f32[1]{0:T(128)}, f32[1]{0:T(128)}, f32[]{:T(128)}, f32[]{:T(128)}) all-reduce(f32[1]{0:T(128)} %bitcast.3, f32[1]{0:T(128)} %bitcast.2, f32[]{:T(128)} %get-tuple-element.21, f32[]{:T(128)} %get-tuple-element.22), channel_id=1, replica_groups=mesh['row_0'=4,'row_1'=4,'row_2'=2,'col'=8] {'col'}, use_global_device_ids=true, to_apply=%region_14.15 | all-reduce | flops 4 | bytes 32 | tf_op jit(solution)/shard_map/psum | solution.py:52
  242.1 1.8 pad_maximum_fusion
  (53 shorter events, 10.9 us)
Async XLA Ops:
  7.2 61.0 %all-gather.3.cloned.1.call-start = ((), (), s32[]{:S(2)}) async-start(), calls=%async_computation.2 | async-start | bytes 6758400 | tf_op jit(solution)/shard_map/all_gather | solution.py:82
  11.8 55.5 %all-to-all-start = ((bf16[8,160,640]{2,1,0:T(8,128)(2,1)}), bf16[8,160,640]{2,1,0:T(8,128)(2,1)S(1)}, u32[]{:S(2)}, u32[]{:S(2)}) async-start(bf16[8,160,640]{2,1,0:T(8,128)(2,1)} %broadcast_in_dim.9), calls=%async_computation | async-start | bytes 3276800 | tf_op jit(solution)/shard_map/all_to_all | solution.py:34
  20.4 143.1 %all-gather.5.cloned.1.call-start = ((), (), s32[]{:S(2)}) async-start(), calls=%async_computation.3 | async-start | bytes 6758400 | tf_op jit(solution)/shard_map/all_gather | solution.py:82
  68.1 32.0 %slice-start.2 = ((s8[6553600]{0:T(1024)(128)(4,1)}), s8[4194304]{0:T(1024)(128)(4,1)S(1)}, s32[]{:S(2)}) async-start(s8[6553600]{0:T(1024)(128)(4,1)} %bitcast.20), calls=%async_computation.6 | async-start | bytes 8388608
  68.3 31.8 %slice-start.3 = ((s8[6553600]{0:T(1024)(128)(4,1)}), s8[2359296]{0:T(1024)(128)(4,1)S(1)}, s32[]{:S(2)}) async-start(s8[6553600]{0:T(1024)(128)(4,1)} %bitcast.20), calls=%async_computation.7 | async-start | bytes 4718592
  72.8 27.3 %copy-start = (bf16[160,640]{1,0:T(8,128)(2,1)S(1)}, bf16[160,640]{1,0:T(8,128)(2,1)}, u32[]{:S(2)}) copy-start(bf16[160,640]{1,0:T(8,128)(2,1)} %get-tuple-element.24) | copy-start | bytes 614404
  72.8 7.3 %collective-permute-start = (bf16[160,640]{1,0:T(8,128)(2,1)S(1)}, bf16[160,640]{1,0:T(8,128)(2,1)S(1)}, u32[]{:S(2)}, u32[]{:S(2)}) collective-permute-start(bf16[160,640]{1,0:T(8,128)(2,1)S(1)} %get-tuple-element.27), channel_id=1, source_target_pairs={{0,1},{1,2},{2,3},{3,4},{4,5},{5,6},{6,7},{7,0},{8,9},{9,10},{10,1... | collective-permute-start | bytes 614408 | tf_op jit(solution)/shard_map/ppermute | solution.py:22
  74.6 7.1 %collective-permute-start.1 = (bf16[160,640]{1,0:T(8,128)(2,1)S(1)}, bf16[160,640]{1,0:T(8,128)(2,1)S(1)}, u32[]{:S(2)}, u32[]{:S(2)}) collective-permute-start(bf16[160,640]{1,0:T(8,128)(2,1)S(1)} %get-tuple-element.27), channel_id=1, source_target_pairs={{0,7},{1,0},{2,1},{3,2},{4,3},{5,4},{6,5},{7,6},{8,15},{9,8},{10,9... | collective-permute-start | bytes 614408 | tf_op jit(solution)/shard_map/ppermute | solution.py:25
  80.1 6.4 %collective-permute-start.2 = (bf16[160,640]{1,0:T(8,128)(2,1)S(1)}, bf16[160,640]{1,0:T(8,128)(2,1)S(1)}, u32[]{:S(2)}, u32[]{:S(2)}) collective-permute-start(bf16[160,640]{1,0:T(8,128)(2,1)S(1)} %collective-permute-done), channel_id=1, source_target_pairs={{0,1},{1,2},{2,3},{3,4},{4,5},{5,6},{6,7},{7,0},{8,9},{9,10},{10,1... | collective-permute-start | bytes 614408 | tf_op jit(solution)/shard_map/ppermute | solution.py:22
  81.7 6.6 %collective-permute-start.3 = (bf16[160,640]{1,0:T(8,128)(2,1)S(1)}, bf16[160,640]{1,0:T(8,128)(2,1)S(1)}, u32[]{:S(2)}, u32[]{:S(2)}) collective-permute-start(bf16[160,640]{1,0:T(8,128)(2,1)S(1)} %collective-permute-done.1), channel_id=1, source_target_pairs={{0,7},{1,0},{2,1},{3,2},{4,3},{5,4},{6,5},{7,6},{8,15},{9,8},{10,9... | collective-permute-start | bytes 614408 | tf_op jit(solution)/shard_map/ppermute | solution.py:25
  86.5 6.4 %collective-permute-start.4 = (bf16[160,640]{1,0:T(8,128)(2,1)S(1)}, bf16[160,640]{1,0:T(8,128)(2,1)S(1)}, u32[]{:S(2)}, u32[]{:S(2)}) collective-permute-start(bf16[160,640]{1,0:T(8,128)(2,1)S(1)} %collective-permute-done.2), channel_id=1, source_target_pairs={{0,1},{1,2},{2,3},{3,4},{4,5},{5,6},{6,7},{7,0},{8,9},{9,10},{10,1... | collective-permute-start | bytes 614408 | tf_op jit(solution)/shard_map/ppermute | solution.py:22
  88.3 6.7 %collective-permute-start.5 = (bf16[160,640]{1,0:T(8,128)(2,1)S(1)}, bf16[160,640]{1,0:T(8,128)(2,1)S(1)}, u32[]{:S(2)}, u32[]{:S(2)}) collective-permute-start(bf16[160,640]{1,0:T(8,128)(2,1)S(1)} %collective-permute-done.3), channel_id=1, source_target_pairs={{0,7},{1,0},{2,1},{3,2},{4,3},{5,4},{6,5},{7,6},{8,15},{9,8},{10,9... | collective-permute-start | bytes 614408 | tf_op jit(solution)/shard_map/ppermute | solution.py:25
  92.9 7.2 %collective-permute-start.6 = (bf16[160,640]{1,0:T(8,128)(2,1)S(1)}, bf16[160,640]{1,0:T(8,128)(2,1)S(1)}, u32[]{:S(2)}, u32[]{:S(2)}) collective-permute-start(bf16[160,640]{1,0:T(8,128)(2,1)S(1)} %collective-permute-done.4), channel_id=1, source_target_pairs={{0,1},{1,2},{2,3},{3,4},{4,5},{5,6},{6,7},{7,0},{8,9},{9,10},{10,1... | collective-permute-start | bytes 614408 | tf_op jit(solution)/shard_map/ppermute | solution.py:22
  163.5 32.8 %slice-start = ((s8[6553600]{0:T(1024)(128)(4,1)}), s8[4194304]{0:T(1024)(128)(4,1)S(1)}, s32[]{:S(2)}) async-start(s8[6553600]{0:T(1024)(128)(4,1)} %bitcast.18), calls=%async_computation.4 | async-start | bytes 8388608
  163.6 32.6 %slice-start.1 = ((s8[6553600]{0:T(1024)(128)(4,1)}), s8[2359296]{0:T(1024)(128)(4,1)S(1)}, s32[]{:S(2)}) async-start(s8[6553600]{0:T(1024)(128)(4,1)} %bitcast.18), calls=%async_computation.5 | async-start | bytes 4718592
  168.1 7.5 %collective-permute-start.7 = (bf16[160,640]{1,0:T(8,128)(2,1)S(1)}, bf16[160,640]{1,0:T(8,128)(2,1)S(1)}, u32[]{:S(2)}, u32[]{:S(2)}) collective-permute-start(bf16[160,640]{1,0:T(8,128)(2,1)S(1)} %get-tuple-element.30), channel_id=1, source_target_pairs={{0,1},{1,2},{2,3},{3,4},{4,5},{5,6},{6,7},{7,0},{8,9},{9,10},{10,1... | collective-permute-start | bytes 614408 | tf_op jit(solution)/shard_map/ppermute | solution.py:22
  169.9 7.2 %collective-permute-start.8 = (bf16[160,640]{1,0:T(8,128)(2,1)S(1)}, bf16[160,640]{1,0:T(8,128)(2,1)S(1)}, u32[]{:S(2)}, u32[]{:S(2)}) collective-permute-start(bf16[160,640]{1,0:T(8,128)(2,1)S(1)} %get-tuple-element.30), channel_id=1, source_target_pairs={{0,7},{1,0},{2,1},{3,2},{4,3},{5,4},{6,5},{7,6},{8,15},{9,8},{10,9... | collective-permute-start | bytes 614408 | tf_op jit(solution)/shard_map/ppermute | solution.py:25
  175.6 6.9 %collective-permute-start.9 = (bf16[160,640]{1,0:T(8,128)(2,1)S(1)}, bf16[160,640]{1,0:T(8,128)(2,1)S(1)}, u32[]{:S(2)}, u32[]{:S(2)}) collective-permute-start(bf16[160,640]{1,0:T(8,128)(2,1)S(1)} %collective-permute-done.7), channel_id=1, source_target_pairs={{0,1},{1,2},{2,3},{3,4},{4,5},{5,6},{6,7},{7,0},{8,9},{9,10},{10,1... | collective-permute-start | bytes 614408 | tf_op jit(solution)/shard_map/ppermute | solution.py:22
  177.2 6.9 %collective-permute-start.10 = (bf16[160,640]{1,0:T(8,128)(2,1)S(1)}, bf16[160,640]{1,0:T(8,128)(2,1)S(1)}, u32[]{:S(2)}, u32[]{:S(2)}) collective-permute-start(bf16[160,640]{1,0:T(8,128)(2,1)S(1)} %collective-permute-done.8), channel_id=1, source_target_pairs={{0,7},{1,0},{2,1},{3,2},{4,3},{5,4},{6,5},{7,6},{8,15},{9,8},{10,9... | collective-permute-start | bytes 614408 | tf_op jit(solution)/shard_map/ppermute | solution.py:25
  182.5 7.0 %collective-permute-start.11 = (bf16[160,640]{1,0:T(8,128)(2,1)S(1)}, bf16[160,640]{1,0:T(8,128)(2,1)S(1)}, u32[]{:S(2)}, u32[]{:S(2)}) collective-permute-start(bf16[160,640]{1,0:T(8,128)(2,1)S(1)} %collective-permute-done.9), channel_id=1, source_target_pairs={{0,1},{1,2},{2,3},{3,4},{4,5},{5,6},{6,7},{7,0},{8,9},{9,10},{10,1... | collective-permute-start | bytes 614408 | tf_op jit(solution)/shard_map/ppermute | solution.py:22
  184.1 6.7 %collective-permute-start.12 = (bf16[160,640]{1,0:T(8,128)(2,1)S(1)}, bf16[160,640]{1,0:T(8,128)(2,1)S(1)}, u32[]{:S(2)}, u32[]{:S(2)}) collective-permute-start(bf16[160,640]{1,0:T(8,128)(2,1)S(1)} %collective-permute-done.10), channel_id=1, source_target_pairs={{0,7},{1,0},{2,1},{3,2},{4,3},{5,4},{6,5},{7,6},{8,15},{9,8},{10,9... | collective-permute-start | bytes 614408 | tf_op jit(solution)/shard_map/ppermute | solution.py:25
  189.5 6.7 %collective-permute-start.13 = (bf16[160,640]{1,0:T(8,128)(2,1)S(1)}, bf16[160,640]{1,0:T(8,128)(2,1)S(1)}, u32[]{:S(2)}, u32[]{:S(2)}) collective-permute-start(bf16[160,640]{1,0:T(8,128)(2,1)S(1)} %collective-permute-done.11), channel_id=1, source_target_pairs={{0,1},{1,2},{2,3},{3,4},{4,5},{5,6},{6,7},{7,0},{8,9},{9,10},{10,1... | collective-permute-start | bytes 614408 | tf_op jit(solution)/shard_map/ppermute | solution.py:22
Sparse Core Ops, SparseCore 0:
  11.1 57.0 all-gather.2
  103.1 60.3 all-gather.4
